TPU v7x, 32 devices: a whole 2x2x4 slice. The times are simulated.
32 devices in a mesh: ep: 4 (over x, core), fsdp: 8 (over z, y).
Axes of the slice: x: 2, y: 2, z: 4, core: 2. Of those that a mesh axis runs over, the one named last changes fastest.
Arguments:
- master_gate: float32 [128, 2048, 768], P('ep', 'fsdp'), may hold values from -0.1875 to 0.1875
- master_up: float32 [128, 2048, 768], P('ep', 'fsdp'), may hold values from -0.1875 to 0.1875
- router_weight: float32 [2048, 128], P('fsdp', 'ep'), may hold values from -0.125 to 0.125
- router_gain: float32 [2048], P('fsdp'), may hold values from 0.25 to 1.75
Outputs:
- final_gate: bfloat16 [128, 2048, 768], P(('ep', 'fsdp'))
- final_up: bfloat16 [128, 2048, 768], P(('ep', 'fsdp'))
- scale_gate: float32 [128, 768], P(('ep', 'fsdp'))
- scale_up: float32 [128, 768], P(('ep', 'fsdp'))
- serve_router: bfloat16 [2048, 128], replicated
All inputs are finite; a program needn't handle non-finite values.
Results may differ from a plain program's by a relative error of at most 0.001.
Values may be sent and summed in bfloat16 or wider, within the bound.
A program may use at most 192 MiB of HBM per device.

v0:
```python
import jax
import jax.numpy as jnp
from jax import lax
from jax.sharding import PartitionSpec as P


def body(master_gate, master_up, router_weight, router_gain):
    total_gate, total_up = lax.psum(
        (jnp.sum(master_gate * master_gate, axis=1), jnp.sum(master_up * master_up, axis=1)), "fsdp"
    )
    scale_gate = jnp.sqrt(total_gate)
    scale_up = jnp.sqrt(total_up)
    narrow_gate, narrow_up = (
        (master_gate / jnp.expand_dims(scale_gate, 1)).astype(jnp.bfloat16),
        (master_up / jnp.expand_dims(scale_up, 1)).astype(jnp.bfloat16),
    )
    final_gate, final_up = (
        lax.all_to_all(narrow_gate, "fsdp", split_axis=0, concat_axis=1, tiled=True),
        lax.all_to_all(narrow_up, "fsdp", split_axis=0, concat_axis=1, tiled=True),
    )
    scale_gate = lax.dynamic_slice_in_dim(
        scale_gate, lax.axis_index("fsdp") * final_gate.shape[0], final_gate.shape[0], axis=0
    )
    scale_up = lax.dynamic_slice_in_dim(
        scale_up, lax.axis_index("fsdp") * final_up.shape[0], final_up.shape[0], axis=0
    )
    part_router = (router_weight * router_gain[:, None]).astype(jnp.bfloat16)
    row_router = lax.all_gather(part_router, "fsdp", axis=0, tiled=True)
    serve_router = lax.all_gather(row_router, "ep", axis=1, tiled=True)
    return (final_gate, final_up, scale_gate, scale_up, serve_router)


def solution(mesh):
    return jax.shard_map(
        body,
        mesh=mesh,
        in_specs=(P("ep", "fsdp", None), P("ep", "fsdp", None), P("fsdp", "ep"), P("fsdp")),
        out_specs=(
            P(("ep", "fsdp"), None, None),
            P(("ep", "fsdp"), None, None),
            P(("ep", "fsdp"), None),
            P(("ep", "fsdp"), None),
            P(),
        ),
        check_vma=False,
    )
```

profile of v0, /device:TPU:0, one launch (start us, length us, event | category | flops | bytes accessed | tf_op | source)
XLA Modules:
  0.0 723.9 jit_solution(15116092223100259474)
XLA Ops:
  7.2 0.0 all-reduce.3.cloned.1.call-start
  7.2 17.3 %multiply_reduce_fusion = (f32[32,768]{1,0:T(8,128)}, f32[32,768]{1,0:T(8,128)}) fusion(f32[32,256,768]{2,1,0:T(8,128)} %param.5, f32[32,256,768]{2,1,0:T(8,128)} %param.4), kind=kLoop, calls=%fused_computation.1 | loop fusion | flops 25116672 | bytes 50528256 | tf_op jit(solution)/shard_map/reduce_sum | solution.py:9
  24.5 0.0 all-reduce.3.cloned.1.call-update
  24.5 73.8 %all-reduce.3.cloned.1.call-done = (f32[32,768]{1,0:T(8,128)}, f32[32,768]{1,0:T(8,128)}) async-done(((f32[32,768]{1,0:T(8,128)}, f32[32,768]{1,0:T(8,128)}), (f32[32,768]{1,0:T(8,128)}, f32[32,768]{1,0:T(8,128)})) %all-reduce.3.cloned.1.call-update) | async-done | bytes 196624 | tf_op jit(solution)/shard_map/psum | solution.py:8
  98.2 0.9 sqrt.6
  99.2 0.0 copy-start
  99.2 13.7 %divide_convert_fusion.1 = bf16[32,256,768]{2,1,0:T(8,128)(2,1)} fusion(f32[32,256,768]{2,1,0:T(8,128)} %param.4, f32[32,768]{1,0:T(8,128)S(1)} %sqrt.6), kind=kLoop, calls=%fused_computation.2 | loop fusion | flops 12582912 | bytes 37847040 | tf_op jit(solution)/shard_map/convert_element_type | solution.py:14
  112.9 5.4 all-to-all-start
  118.2 0.0 copy-done
  118.3 0.0 copy-start.1
  118.3 0.0 copy-start.2
  118.3 13.8 %divide_convert_fusion = bf16[32,256,768]{2,1,0:T(8,128)(2,1)} fusion(f32[32,256,768]{2,1,0:T(8,128)} %param.5, f32[32,768]{1,0:T(8,128)S(1)} %sqrt.7), kind=kLoop, calls=%fused_computation | loop fusion | flops 12582912 | bytes 37847040 | tf_op jit(solution)/shard_map/convert_element_type | solution.py:15
  132.1 257.3 %all-to-all-done = bf16[32,256,768]{2,1,0:T(8,128)(2,1)} async-done(((bf16[32,256,768]{2,1,0:T(8,128)(2,1)}), bf16[32,256,768]{2,1,0:T(8,128)(2,1)}, u32[]{:S(2)}, u32[]{:S(2)}) %all-to-all-start) | async-done | bytes 12582944 | tf_op jit(solution)/shard_map/all_to_all | solution.py:18
  389.4 5.4 all-to-all-start.1
  394.8 0.0 copy-done.1
  394.8 0.0 copy-done.2
  394.8 291.6 %all_gather.6 = bf16[2048,32]{0,1:T(8,128)(2,1)S(1)} all-gather(bf16[256,32]{0,1:T(8,128)(2,1)S(1)} %multiply_convert_fusion), channel_id=1, replica_groups=mesh['ep'=4,'fsdp'=8] {'fsdp'}, dimensions={0}, use_global_device_ids=true | all-gather | bytes 147456 | tf_op jit(solution)/shard_map/all_gather | solution.py:28
  686.4 7.1 all_gather.7
  693.5 1.0 copy.14
  694.5 0.6 constant_dynamic-slice_fusion
  695.1 0.6 constant_dynamic-slice_fusion.1
  695.7 10.7 %copy.12 = bf16[8,4,256,768]{3,2,0,1:T(8,128)(2,1)} copy(bf16[8,4,256,768]{3,2,1,0:T(8,128)(2,1)} %bitcast) | data formatting | bytes 25165824 | tf_op jit(solution)/shard_map/all_to_all | solution.py:18
  706.4 0.0 all-to-all-done.1
  706.4 10.7 %copy.13 = bf16[8,4,256,768]{3,2,0,1:T(8,128)(2,1)} copy(bf16[8,4,256,768]{3,2,1,0:T(8,128)(2,1)} %bitcast.3) | data formatting | bytes 25165824 | tf_op jit(solution)/shard_map/all_to_all | solution.py:19
  (2 shorter events, 0.0 us)
Async XLA Ops:
  7.2 91.1 %all-reduce.3.cloned.1.call-start = ((), (), s32[]{:S(2)}) async-start(), calls=%async_computation.2 | async-start | bytes 393216 | tf_op jit(solution)/shard_map/psum | solution.py:8
  99.2 19.1 %copy-start = (f32[32,768]{1,0:T(8,128)S(1)}, f32[32,768]{1,0:T(8,128)}, u32[]{:S(2)}) copy-start(f32[32,768]{1,0:T(8,128)} %get-tuple-element.11) | copy-start | bytes 294916
  112.9 276.5 %all-to-all-start = ((bf16[32,256,768]{2,1,0:T(8,128)(2,1)}), bf16[32,256,768]{2,1,0:T(8,128)(2,1)}, u32[]{:S(2)}, u32[]{:S(2)}) async-start(bf16[32,256,768]{2,1,0:T(8,128)(2,1)} %divide_convert_fusion.1), calls=%async_computation | async-start | bytes 25165824 | tf_op jit(solution)/shard_map/all_to_all | solution.py:18
  118.3 276.5 %copy-start.1 = (f32[256,32]{0,1:T(8,128)S(1)}, f32[256,32]{0,1:T(8,128)}, u32[]{:S(2)}) copy-start(f32[256,32]{0,1:T(8,128)} %param.6) | copy-start | bytes 98308
  118.3 276.5 %copy-start.2 = (f32[256]{0:T(256)S(1)}, f32[256]{0:T(256)}, u32[]{:S(2)}) copy-start(f32[256]{0:T(256)} %param.7) | copy-start | bytes 3076
  389.4 317.0 %all-to-all-start.1 = ((bf16[32,256,768]{2,1,0:T(8,128)(2,1)}), bf16[32,256,768]{2,1,0:T(8,128)(2,1)}, u32[]{:S(2)}, u32[]{:S(2)}) async-start(bf16[32,256,768]{2,1,0:T(8,128)(2,1)} %divide_convert_fusion), calls=%async_computation.1 | async-start | bytes 25165824 | tf_op jit(solution)/shard_map/all_to_all | solution.py:19
Sparse Core Ops, SparseCore 0:
  24.6 73.5 all-reduce.2
where the time goes:
time: 724 us
  waiting for transfers between devices  331 us (46%)
  blocking collectives  299 us (41%)
  other arithmetic  44.7 us (6%)
  local copies, waits for them, and re-layouts  24.5 us (3%)
  between operations  14.1 us (2%)
  starting transfers between devices  10.8 us (1%)
    all_gather x1, blocking collectives, body(): row_router = lax.all_gather(part_router, 'fsdp', axis=0, tiled=True)  292 us
    all_to_all x1, waiting for transfers between devices, body(): lax.all_to_all(narrow_gate, 'fsdp', split_axis=0, concat_axis=1, tiled=True)  257 us
    psum x1, waiting for transfers between devices, body(): lax.psum((jnp.sum(master_gate * master_gate, axis=1), jnp.sum(master_up *...  73.8 us
    reduce_sum x1, other arithmetic, body(): jnp.sum(master_up * master_up, axis=1)  17.3 us
  transfers between devices with their start and end apart: 3, of which 2 were waited for; matrix products, arithmetic and copies ran while one was open for 4% of the time, Pallas kernels for 0%

commit v1 on v0

--- a/solution.py
+++ b/solution.py
@@ -25,7 +25,12 @@
         scale_up, lax.axis_index("fsdp") * final_up.shape[0], final_up.shape[0], axis=0
     )
     part_router = (router_weight * router_gain[:, None]).astype(jnp.bfloat16)
-    row_router = lax.all_gather(part_router, "fsdp", axis=0, tiled=True)
+    ring = [part_router]
+    for hop in range(7):
+        ring.append(lax.ppermute(ring[-1], "fsdp", [(dev, (dev + 1) % 8) for dev in range(8)]))
+    row_router = jnp.roll(
+        jnp.concatenate(ring[::-1], axis=0), (lax.axis_index("fsdp") + 1) * ring[0].shape[0], axis=0
+    )
     serve_router = lax.all_gather(row_router, "ep", axis=1, tiled=True)
     return (final_gate, final_up, scale_gate, scale_up, serve_router)
 

time: 724 us -> 730 us (level)
  blocking collectives: 299 us -> 7.15 us
  waiting for transfers between devices: 331 us -> 565 us
  starting transfers between devices: 10.8 us -> 73.9 us
    all_gather x1 -> x0, blocking collectives: 292 us -> none  [body(): row_router = lax.all_gather(part_router, 'fsdp', axis=0, tiled=True)]
    ppermute x0 -> x7, waiting for transfers between devices: none -> 234 us  [body(): lax.ppermute(ring[-1], 'fsdp', [(dev, (dev + 1) % 8) for dev in range(8)])]
    ppermute x0 -> x7, starting transfers between devices: none -> 63.1 us  [body(): lax.ppermute(ring[-1], 'fsdp', [(dev, (dev + 1) % 8) for dev in range(8)])]
  transfers between devices with their start and end apart: 3 -> 10, of which waited for: 2 -> 9; matrix products, arithmetic and copies ran while one was open for 4% -> 4% of each run, Pallas kernels for 0% -> 0%
where the time goes in v1:
time: 730 us
  waiting for transfers between devices  565 us (77%)
  starting transfers between devices  73.9 us (10%)
  other arithmetic  44.8 us (6%)
  local copies, waits for them, and re-layouts  24.6 us (3%)
  between operations  14.2 us (2%)
    all_to_all x1, waiting for transfers between devices, body(): lax.all_to_all(narrow_gate, 'fsdp', split_axis=0, concat_axis=1, tiled=True)  257 us
    ppermute x7, waiting for transfers between devices, body(): lax.ppermute(ring[-1], 'fsdp', [(dev, (dev + 1) % 8) for dev in range(8)])  234 us
    psum x1, waiting for transfers between devices, body(): lax.psum((jnp.sum(master_gate * master_gate, axis=1), jnp.sum(master_up *...  73.8 us
    ppermute x7, starting transfers between devices, body(): lax.ppermute(ring[-1], 'fsdp', [(dev, (dev + 1) % 8) for dev in range(8)])  63.1 us
    reduce_sum x1, other arithmetic, body(): jnp.sum(master_up * master_up, axis=1)  17.3 us
  transfers between devices with their start and end apart: 10, of which 9 were waited for; matrix products, arithmetic and copies ran while one was open for 4% of the time, Pallas kernels for 0%

profile of v1, /device:TPU:0, one launch (start us, length us, event | category | flops | bytes accessed | tf_op | source)
XLA Modules:
  0.0 729.9 jit_solution(6185651986433440676)
XLA Ops:
  7.2 0.0 all-reduce.3.cloned.1.call-start
  7.2 17.3 %multiply_reduce_fusion = (f32[32,768]{1,0:T(8,128)}, f32[32,768]{1,0:T(8,128)}) fusion(f32[32,256,768]{2,1,0:T(8,128)} %param.5, f32[32,256,768]{2,1,0:T(8,128)} %param.4), kind=kLoop, calls=%fused_computation.1 | loop fusion | flops 25116672 | bytes 50528256 | tf_op jit(solution)/shard_map/reduce_sum | solution.py:9
  24.5 0.0 all-reduce.3.cloned.1.call-update
  24.5 73.8 %all-reduce.3.cloned.1.call-done = (f32[32,768]{1,0:T(8,128)}, f32[32,768]{1,0:T(8,128)}) async-done(((f32[32,768]{1,0:T(8,128)}, f32[32,768]{1,0:T(8,128)}), (f32[32,768]{1,0:T(8,128)}, f32[32,768]{1,0:T(8,128)})) %all-reduce.3.cloned.1.call-update) | async-done | bytes 196624 | tf_op jit(solution)/shard_map/psum | solution.py:8
  98.2 0.9 sqrt.6
  99.2 0.0 copy-start.1
  99.2 13.7 %divide_convert_fusion.1 = bf16[32,256,768]{2,1,0:T(8,128)(2,1)} fusion(f32[32,256,768]{2,1,0:T(8,128)} %param.4, f32[32,768]{1,0:T(8,128)S(1)} %sqrt.6), kind=kLoop, calls=%fused_computation.2 | loop fusion | flops 12582912 | bytes 37847040 | tf_op jit(solution)/shard_map/convert_element_type | solution.py:14
  112.9 5.3 all-to-all-start
  118.2 0.0 copy-done.1
  118.2 0.0 copy-start
  118.3 0.0 copy-start.2
  118.3 13.9 %divide_convert_fusion = bf16[32,256,768]{2,1,0:T(8,128)(2,1)} fusion(f32[32,256,768]{2,1,0:T(8,128)} %param.5, f32[32,768]{1,0:T(8,128)S(1)} %sqrt.7), kind=kLoop, calls=%fused_computation | loop fusion | flops 12582912 | bytes 37847040 | tf_op jit(solution)/shard_map/convert_element_type | solution.py:15
  132.1 257.2 %all-to-all-done = bf16[32,256,768]{2,1,0:T(8,128)(2,1)} async-done(((bf16[32,256,768]{2,1,0:T(8,128)(2,1)}), bf16[32,256,768]{2,1,0:T(8,128)(2,1)}, u32[]{:S(2)}, u32[]{:S(2)}) %all-to-all-start) | async-done | bytes 12582944 | tf_op jit(solution)/shard_map/all_to_all | solution.py:18
  389.4 5.3 all-to-all-start.1
  394.7 0.0 copy-done
  394.7 0.0 copy-done.2
  394.8 1.9 collective-permute-start
  396.7 204.3 %collective-permute-done = bf16[256,32]{0,1:T(8,128)(2,1)S(1)} collective-permute-done((bf16[256,32]{0,1:T(8,128)(2,1)S(1)}, bf16[256,32]{0,1:T(8,128)(2,1)S(1)}, u32[]{:S(2)}, u32[]{:S(2)}) %collective-permute-start) | collective-permute-done | bytes 16416 | tf_op jit(solution)/shard_map/ppermute | solution.py:30
  601.0 0.0 collective-permute-start.1
  601.0 6.5 collective-permute-done.1
  607.5 24.0 %collective-permute-start.2 = (bf16[256,32]{0,1:T(8,128)(2,1)S(1)}, bf16[256,32]{0,1:T(8,128)(2,1)S(1)}, u32[]{:S(2)}, u32[]{:S(2)}) collective-permute-start(bf16[256,32]{0,1:T(8,128)(2,1)S(1)} %collective-permute-done.1), channel_id=1, source_target_pairs={{0,1},{1,2},{2,3},{3,4},{4,5},{5,6},{6,7},{7,0},{8,9},{9,10},{10,1... | collective-permute-start | bytes 49160 | tf_op jit(solution)/shard_map/ppermute | solution.py:30
  631.5 6.7 collective-permute-done.2
  638.2 32.7 %collective-permute-start.3 = (bf16[256,32]{0,1:T(8,128)(2,1)S(1)}, bf16[256,32]{0,1:T(8,128)(2,1)S(1)}, u32[]{:S(2)}, u32[]{:S(2)}) collective-permute-start(bf16[256,32]{0,1:T(8,128)(2,1)S(1)} %collective-permute-done.2), channel_id=1, source_target_pairs={{0,1},{1,2},{2,3},{3,4},{4,5},{5,6},{6,7},{7,0},{8,9},{9,10},{10,1... | collective-permute-start | bytes 49160 | tf_op jit(solution)/shard_map/ppermute | solution.py:30
  670.9 1.4 collective-permute-done.3
  672.4 3.4 collective-permute-start.4
  675.8 3.5 collective-permute-done.4
  679.3 1.1 collective-permute-start.5
  680.4 5.3 collective-permute-done.5
  685.7 0.0 collective-permute-start.6
  685.7 6.4 collective-permute-done.6
  692.3 7.1 all_gather.3
  699.5 1.0 copy.14
  700.5 0.6 constant_dynamic-slice_fusion.2
  701.1 0.6 constant_dynamic-slice_fusion.1
  701.7 10.7 %copy.12 = bf16[8,4,256,768]{3,2,0,1:T(8,128)(2,1)} copy(bf16[8,4,256,768]{3,2,1,0:T(8,128)(2,1)} %bitcast) | data formatting | bytes 25165824 | tf_op jit(solution)/shard_map/all_to_all | solution.py:18
  712.4 0.0 all-to-all-done.1
  712.4 10.7 %copy.13 = bf16[8,4,256,768]{3,2,0,1:T(8,128)(2,1)} copy(bf16[8,4,256,768]{3,2,1,0:T(8,128)(2,1)} %bitcast.3) | data formatting | bytes 25165824 | tf_op jit(solution)/shard_map/all_to_all | solution.py:19
  (19 shorter events, 0.1 us)
Async XLA Ops:
  7.2 91.1 %all-reduce.3.cloned.1.call-start = ((), (), s32[]{:S(2)}) async-start(), calls=%async_computation.2 | async-start | bytes 393216 | tf_op jit(solution)/shard_map/psum | solution.py:8
  99.2 19.0 %copy-start.1 = (f32[32,768]{1,0:T(8,128)S(1)}, f32[32,768]{1,0:T(8,128)}, u32[]{:S(2)}) copy-start(f32[32,768]{1,0:T(8,128)} %get-tuple-element.11) | copy-start | bytes 294916
  112.9 276.5 %all-to-all-start = ((bf16[32,256,768]{2,1,0:T(8,128)(2,1)}), bf16[32,256,768]{2,1,0:T(8,128)(2,1)}, u32[]{:S(2)}, u32[]{:S(2)}) async-start(bf16[32,256,768]{2,1,0:T(8,128)(2,1)} %divide_convert_fusion.1), calls=%async_computation | async-start | bytes 25165824 | tf_op jit(solution)/shard_map/all_to_all | solution.py:18
  118.2 276.5 %copy-start = (f32[256,32]{0,1:T(8,128)S(1)}, f32[256,32]{0,1:T(8,128)}, u32[]{:S(2)}) copy-start(f32[256,32]{0,1:T(8,128)} %param.6) | copy-start | bytes 98308
  118.3 276.5 %copy-start.2 = (f32[256]{0:T(256)S(1)}, f32[256]{0:T(256)}, u32[]{:S(2)}) copy-start(f32[256]{0:T(256)} %param.7) | copy-start | bytes 3076
  389.4 323.0 %all-to-all-start.1 = ((bf16[32,256,768]{2,1,0:T(8,128)(2,1)}), bf16[32,256,768]{2,1,0:T(8,128)(2,1)}, u32[]{:S(2)}, u32[]{:S(2)}) async-start(bf16[32,256,768]{2,1,0:T(8,128)(2,1)} %divide_convert_fusion), calls=%async_computation.1 | async-start | bytes 25165824 | tf_op jit(solution)/shard_map/all_to_all | solution.py:19
  394.8 206.2 %collective-permute-start = (bf16[256,32]{0,1:T(8,128)(2,1)S(1)}, bf16[256,32]{0,1:T(8,128)(2,1)S(1)}, u32[]{:S(2)}, u32[]{:S(2)}) collective-permute-start(bf16[256,32]{0,1:T(8,128)(2,1)S(1)} %multiply_convert_fusion), channel_id=1, source_target_pairs={{0,1},{1,2},{2,3},{3,4},{4,5},{5,6},{6,7},{7,0},{8,9},{9,10},{10,1... | collective-permute-start | bytes 49160 | tf_op jit(solution)/shard_map/ppermute | solution.py:30
  601.0 6.5 collective-permute-start.1
  607.5 30.7 %collective-permute-start.2 = (bf16[256,32]{0,1:T(8,128)(2,1)S(1)}, bf16[256,32]{0,1:T(8,128)(2,1)S(1)}, u32[]{:S(2)}, u32[]{:S(2)}) collective-permute-start(bf16[256,32]{0,1:T(8,128)(2,1)S(1)} %collective-permute-done.1), channel_id=1, source_target_pairs={{0,1},{1,2},{2,3},{3,4},{4,5},{5,6},{6,7},{7,0},{8,9},{9,10},{10,1... | collective-permute-start | bytes 49160 | tf_op jit(solution)/shard_map/ppermute | solution.py:30
  638.2 34.1 %collective-permute-start.3 = (bf16[256,32]{0,1:T(8,128)(2,1)S(1)}, bf16[256,32]{0,1:T(8,128)(2,1)S(1)}, u32[]{:S(2)}, u32[]{:S(2)}) collective-permute-start(bf16[256,32]{0,1:T(8,128)(2,1)S(1)} %collective-permute-done.2), channel_id=1, source_target_pairs={{0,1},{1,2},{2,3},{3,4},{4,5},{5,6},{6,7},{7,0},{8,9},{9,10},{10,1... | collective-permute-start | bytes 49160 | tf_op jit(solution)/shard_map/ppermute | solution.py:30
  672.4 6.9 collective-permute-start.4
  679.3 6.4 collective-permute-start.5
  685.7 6.4 collective-permute-start.6
Sparse Core Ops, SparseCore 0:
  24.6 73.5 all-reduce.2
